TPU v7x, 128 devices: a whole 4x4x4 slice. The times are simulated.
128 devices in a mesh: wide: 64 (over y, z, x), narrow: 2 (over core).
Axes of the slice: x: 4, y: 4, z: 4, core: 2. Of those that a mesh axis runs over, the one named last changes fastest.
Arguments:
- tokens: bfloat16 [16384, 4096], P(('wide', 'narrow')), may hold values from -6 to 6
- expert_ids: int32 [16384, 2], P(('wide', 'narrow')), may hold values from 0 to 127, all different within a row; in each aligned block of 128 rows (0 to 127, 128 to 255, ...) at most 3 rows name the same one
- gate_values: bfloat16 [16384, 2], P(('wide', 'narrow')), may hold values from 0.099609375 to 1
- capacity: int32 [128], replicated, may hold values from 128 to 383
- w_gate: bfloat16 [128, 4096, 768], P(('wide', 'narrow')), may hold values from -0.09375 to 0.09375
- w_up: bfloat16 [128, 4096, 768], P(('wide', 'narrow')), may hold values from -0.09375 to 0.09375
- w_down: bfloat16 [128, 768, 4096], P(('wide', 'narrow')), may hold values from -0.21875 to 0.21875
Outputs:
- mixed: bfloat16 [16384, 4096], P(('wide', 'narrow'))
Inputs may be any that keep to these rules, and one draw needn't show every extreme that they name: `expert_ids`: the two experts of a token differ; among the tokens of one device no expert is named more than 3 times, and that many is reached.
All inputs are finite; a program needn't handle non-finite values.
Results may differ from a plain program's by a relative error of at most 0.0058.
Values may be sent and summed in bfloat16 or wider, within the bound.
No kernel may reach another device: no remote copies, remote signals or barrier semaphores. Data moves between devices by JAX's collectives and lax.ppermute only.
A program may use at most 128 MiB of HBM per device.

v0:
```python
import jax
import jax.numpy as jnp
from jax import lax
from jax.sharding import Mesh
from jax.sharding import PartitionSpec as P

WIDE = ("wide_0", "wide_1", "wide_2")
WIDE_NARROW = ("wide_0", "wide_1", "wide_2", "narrow")


def nothing_yet(value, identity):
    return jnp.zeros_like(value) + jnp.asarray(identity, value.dtype)


def carried_in(value, axes, combine, identity):
    before = start = nothing_yet(value, identity)
    so_far = value
    for axis in reversed(axes):
        length, index = (lax.axis_size(axis), lax.axis_index(axis))
        pieces = lax.all_gather(so_far, axis)
        inside, so_far = (start, start)
        for k in range(length):
            passed = k < index
            so_far = combine(so_far, pieces[k])
            inside = jnp.where(passed, so_far, inside)
        before = combine(inside, before)
    return before


def cut_along(value, dim, length):
    before, after = (value.shape[:dim], value.shape[dim + 1 :])
    return jnp.moveaxis(value.reshape(*before, length, -1, *after), dim, 0)


def laid_out(blocks, dim):
    blocks = jnp.moveaxis(blocks, 0, dim)
    dims = blocks.shape
    return blocks.reshape(*dims[:dim], dims[dim] * dims[dim + 1], *dims[dim + 2 :])


def exchange_both(value, axis, axes, splits, concats):
    sizes = [lax.axis_size(a) for a in axes]
    blocks = cut_along(value, splits[0], sizes[0])
    blocks = jnp.moveaxis(cut_along(blocks, splits[1] + 1, sizes[1]), 0, 1)
    inside = blocks.shape[2:]
    blocks = blocks.reshape(-1, *inside)
    blocks = lax.all_to_all(blocks, axis, split_axis=0, concat_axis=0, tiled=True)
    blocks = laid_out(blocks.reshape(*sizes, *inside), concats[0] + 1)
    return laid_out(blocks, concats[1])


def expert_apply(token_rows, gate_matrix, up_matrix, down_matrix):
    gate_part = jnp.dot(token_rows, gate_matrix, preferred_element_type=jnp.float32)
    up_part = jnp.dot(token_rows, up_matrix, preferred_element_type=jnp.float32)
    hidden = (jax.nn.silu(gate_part) * up_part).astype(jnp.bfloat16)
    return jnp.dot(hidden, down_matrix, preferred_element_type=jnp.float32).astype(jnp.bfloat16)


def add_counts(earlier, later):
    return earlier + later


def on_device(tokens, expert_ids, gate_values, capacity, w_gate, w_up, w_down):
    experts = capacity.shape[0]
    tok_rows = tokens.shape[0]
    width = tokens.shape[1]
    most_rows = 3 * tok_rows // experts
    wide_count = lax.axis_size(WIDE)
    narrow_count = lax.axis_size("narrow")
    flat_ids = expert_ids.reshape(-1)
    onehot = (flat_ids[:, None] == jnp.arange(experts, dtype=jnp.int32)[None, :]).astype(jnp.int32)
    local_counts = jnp.sum(onehot, axis=0)
    earlier_counts = carried_in(
        local_counts, WIDE_NARROW, add_counts, jnp.zeros((experts,), jnp.int32)
    )
    local_rank = jnp.sum((jnp.cumsum(onehot, axis=0) - onehot) * onehot, axis=1)
    global_rank = local_rank + jnp.sum(onehot * earlier_counts[None, :], axis=1)
    limit = jnp.sum(onehot * capacity[None, :], axis=1)
    kept_mask = global_rank < limit
    slot_index = flat_ids * most_rows + local_rank
    token_rows = jnp.repeat(tokens, 2, axis=0)
    token_rows = jnp.where(kept_mask[:, None], token_rows, jnp.zeros_like(token_rows))
    outgoing = jnp.zeros((experts * most_rows, width), jnp.bfloat16).at[slot_index].set(token_rows)
    gate_matrix = w_gate[0]
    up_matrix = w_up[0]
    down_matrix = w_down[0]
    outgoing = outgoing.reshape(wide_count, narrow_count, most_rows, width)
    arrived = lax.all_to_all(
        lax.all_to_all(outgoing, WIDE, split_axis=0, concat_axis=0, tiled=True),
        "narrow",
        split_axis=1,
        concat_axis=1,
        tiled=True,
    )
    results = expert_apply(arrived.reshape(-1, width), gate_matrix, up_matrix, down_matrix)
    results = results.reshape(wide_count, narrow_count, most_rows, width)
    answers = exchange_both(results, WIDE_NARROW, (WIDE, "narrow"), (0, 1), (0, 1))
    answers = answers.reshape(experts * most_rows, width)
    picked = answers[slot_index]
    weights = gate_values.reshape(-1).astype(jnp.float32) * kept_mask.astype(jnp.float32)
    scaled = picked.astype(jnp.float32) * weights[:, None]
    mixed = jnp.sum(scaled.reshape(tok_rows, 2, width), axis=1)
    return mixed.astype(jnp.bfloat16)


def solution(mesh):
    finer = Mesh(
        mesh.devices.reshape(4, 4, 4, mesh.shape["narrow"]),
        ("wide_0", "wide_1", "wide_2", "narrow"),
    )
    placed = (
        P(WIDE_NARROW, None),
        P(WIDE_NARROW, None),
        P(WIDE_NARROW, None),
        P(),
        P(WIDE_NARROW, None, None),
        P(WIDE_NARROW, None, None),
        P(WIDE_NARROW, None, None),
    )
    return jax.shard_map(
        on_device, mesh=finer, in_specs=placed, out_specs=P(WIDE_NARROW, None), check_vma=False
    )
```

profile of v0, /device:TPU:1, one launch (start us, length us, event | category | flops | bytes accessed | tf_op | source)
XLA Modules:
  0.0 226.2 jit_solution(11430728936010190123)
XLA Ops:
  0.0 0.8 copy.16
  0.8 0.1 eq.25
  0.9 0.1 eq.29
  1.1 0.7 broadcast_multiply_fusion
  1.8 0.1 convert_reduce_fusion
  1.9 2.8 %all-gather.2 = s32[2,1,128]{2,1,0:T(1,128)S(1)} all-gather(s32[1,1,128]{2,1,0:T(1,128)S(1)} %bitcast.68), channel_id=2, replica_groups=mesh['wide_0'=4,'wide_1'=4,'wide_2'=4,'narrow'=2] {'narrow'}, dimensions={0}, use_global_device_ids=true | all-gather | bytes 1536 | tf_op jit(solution)/shard_map/all_gather | solution.py:20
  4.7 7.8 %all-gather.3 = s32[4,1,128]{2,1,0:T(1,128)S(1)} all-gather(s32[1,1,128]{2,1,0:T(1,128)S(1)} %slice_add_fusion.9), channel_id=3, replica_groups=mesh['wide_0'=4,'wide_1'=4,'wide_2'=4,'narrow'=2] {'wide_2'}, dimensions={0}, use_global_device_ids=true | all-gather | bytes 2560 | tf_op jit(solution)/shard_map/all_gather | solution.py:20
  12.5 9.0 %all-gather.4 = s32[4,1,128]{2,1,0:T(1,128)S(1)} all-gather(s32[1,1,128]{2,1,0:T(1,128)S(1)} %slice_add_fusion.6), channel_id=1, replica_groups=mesh['wide_0'=4,'wide_1'=4,'wide_2'=4,'narrow'=2] {'wide_1'}, dimensions={0}, use_global_device_ids=true | all-gather | bytes 2560 | tf_op jit(solution)/shard_map/all_gather | solution.py:20
  21.5 7.9 %all-gather.5 = s32[4,1,128]{2,1,0:T(1,128)S(1)} all-gather(s32[1,1,128]{2,1,0:T(1,128)S(1)} %slice_add_fusion.3), channel_id=1, replica_groups=mesh['wide_0'=4,'wide_1'=4,'wide_2'=4,'narrow'=2] {'wide_0'}, dimensions={0}, use_global_device_ids=true | all-gather | bytes 2560 | tf_op jit(solution)/shard_map/all_gather | solution.py:20
  29.5 0.1 copy.18
  29.6 0.2 fusion.25
  29.9 0.1 copy.15
  30.0 0.1 mul.58
  30.1 0.0 copy-start
  30.1 3.3 %broadcast_in_dim.30 = bf16[128,2,4096]{2,1,0:T(2,128)(2,1)S(1)} broadcast(bf16[128,4096]{1,0:T(8,128)(2,1)} %param.7), dimensions={0,2} | broadcast | bytes 3145728 | tf_op jit(solution)/shard_map/broadcast_in_dim | solution.py:81
  33.5 2.2 reshape.97
  35.7 0.0 copy-done
  35.7 0.3 select_reduce_fusion.1
  36.0 5.6 %scatter_custom_fusion = bf16[384,4096]{1,0:T(8,128)(2,1)S(1)} fusion(s32[256]{0:T(256)S(1)} %bitcast.66, bf16[256,4096]{1,0:T(8,128)(2,1)} %reshape.97, pred[256]{0:T(512)(128)(4,1)S(1)} %add_compare_fusion, bf16[]{:T(256)} %constant.14.clone.1), kind=kCustom, calls=%fused_computation.10 | custom fusion | flops 1048576 | bytes 5244416 | tf_op jit(solution)/shard_map/scatter | solution.py:83
  41.6 4.4 %reshape.98 = bf16[64,2,3,4096]{3,2,1,0:T(4,128)(2,1)} reshape(bf16[384,4096]{1,0:T(8,128)(2,1)S(1)} %scatter_custom_fusion) | data formatting | bytes 6291456 | tf_op jit(solution)/shard_map/reshape | solution.py:87
  46.0 6.4 %copy.20 = bf16[64,2,3,4096]{3,1,2,0:T(2,128)(2,1)S(1)} copy(bf16[64,2,3,4096]{3,2,1,0:T(4,128)(2,1)} %reshape.98) | data formatting | bytes 6291456 | tf_op jit(solution)/shard_map/reshape | solution.py:87
  52.4 39.4 %all_to_all.15 = bf16[64,2,3,4096]{3,1,2,0:T(2,128)(2,1)S(1)} all-to-all(bf16[64,2,3,4096]{3,1,2,0:T(2,128)(2,1)S(1)} %copy.20), channel_id=1, replica_groups=mesh['wide_0'=4,'wide_1'=4,'wide_2'=4,'narrow'=2] {'wide_0','wide_1','wi..., dimensions={0} | all-to-all | bytes 6291456 | tf_op jit(solution)/shard_map/all_to_all | solution.py:89
  91.9 2.1 copy.21
  94.0 12.8 %all_to_all.16 = bf16[64,2,3,4096]{3,0,2,1:T(8,128)(2,1)S(1)} all-to-all(bf16[64,2,3,4096]{3,0,2,1:T(8,128)(2,1)S(1)} %copy.21), channel_id=1, replica_groups=mesh['wide_0'=4,'wide_1'=4,'wide_2'=4,'narrow'=2] {'narrow'}, dimensions={1} | all-to-all | bytes 6291456 | tf_op jit(solution)/shard_map/all_to_all | solution.py:88
  106.8 4.6 %copy.22 = bf16[64,2,3,4096]{3,2,1,0:T(4,128)(2,1)} copy(bf16[64,2,3,4096]{3,0,2,1:T(8,128)(2,1)S(1)} %all_to_all.16) | data formatting | bytes 6291456 | tf_op jit(solution)/shard_map/all_to_all | solution.py:88
  111.4 6.0 %reshape.99 = bf16[384,4096]{1,0:T(8,128)(2,1)S(1)} reshape(bf16[64,2,3,4096]{3,2,1,0:T(4,128)(2,1)} %copy.22) | data formatting | bytes 6291456 | tf_op jit(solution)/shard_map/reshape | solution.py:95
  117.4 6.4 %fusion.4 = f32[384,768]{1,0:T(8,128)} fusion(bf16[384,4096]{1,0:T(8,128)(2,1)S(1)} %reshape.99, bf16[1,4096,768]{2,1,0:T(8,128)(2,1)} %param.11), kind=kOutput, calls=%fused_computation.6 | convolution fusion | flops 2415919104 | bytes 10616832 | tf_op jit(solution)/shard_map/dot_general | solution.py:53
  123.8 13.3 %fusion.6 = bf16[384,4096]{1,0:T(8,128)(2,1)} fusion(bf16[1,768,4096]{2,1,0:T(8,128)(2,1)} %param.13, bf16[384,4096]{1,0:T(8,128)(2,1)S(1)} %reshape.99, bf16[1,4096,768]{2,1,0:T(8,128)(2,1)} %param.12, f32[384,768]{1,0:T(8,128)} %fusion.4), kind=kOutput, calls=%fused_computation.8 | convolution fusion | flops 4835180544 | bytes 20054016 | tf_op jit(solution)/shard_map/dot_general | solution.py:56
  137.1 7.1 %reshape_transpose_transpose_reshape_reshape_reshape.3 = bf16[128,1,1,3,4096]{4,3,0,2,1:T(4,128)(2,1)} reshape(bf16[384,4096]{1,0:T(8,128)(2,1)} %fusion.6) | data formatting | bytes 6291456 | tf_op jit(solution)/shard_map/reshape;transpose;transpose;reshape;reshape;reshape | solution.py:46
  144.2 0.0 copy-start.1
  144.2 5.1 %all-to-all-start.2 = ((bf16[128,1,1,3,4096]{4,3,2,1,0:T(4,128)(2,1)}), bf16[128,1,1,3,4096]{4,3,2,1,0:T(4,128)(2,1)}, u32[]{:S(2)}, u32[]{:S(2)}) async-start(bf16[128,1,1,3,4096]{4,3,2,1,0:T(4,128)(2,1)} %bitcast.61), calls=%async_computation.2 | async-start | bytes 8388608 | tf_op jit(solution)/shard_map/all_to_all | solution.py:47
  149.3 0.2 lt.26
  149.5 0.0 copy-done.1
  149.5 0.1 copy.24
  149.6 52.3 %all-to-all-done.2 = bf16[128,1,1,3,4096]{4,3,2,1,0:T(4,128)(2,1)} async-done(((bf16[128,1,1,3,4096]{4,3,2,1,0:T(4,128)(2,1)}), bf16[128,1,1,3,4096]{4,3,2,1,0:T(4,128)(2,1)}, u32[]{:S(2)}, u32[]{:S(2)}) %all-to-all-start.2) | async-done | bytes 3145760 | tf_op jit(solution)/shard_map/all_to_all | solution.py:47
  202.0 6.0 %reshape_reshape.3 = bf16[384,4096]{1,0:T(8,128)(2,1)S(1)} reshape(bf16[64,2,1,3,4096]{4,3,1,0,2:T(4,128)(2,1)} %bitcast.21) | data formatting | bytes 6291456 | tf_op jit(solution)/shard_map/reshape;reshape | solution.py:98
  207.9 3.2 %gather_fusion = bf16[256,4096]{1,0:T(8,128)(2,1)} fusion(bf16[384,4096]{1,0:T(8,128)(2,1)S(1)} %reshape_reshape.3, s32[1024]{0:T(1024)S(1)} %pad_clamp_fusion), kind=kCustom, calls=%fused_computation | custom fusion | bytes 4195328 | tf_op jit(solution)/shard_map/gather | solution.py:99
  211.1 5.4 %reshape.102 = f32[128,2,4096]{2,1,0:T(2,128)} reshape(bf16[256,4096]{1,0:T(8,128)(2,1)} %gather_fusion) | data formatting | bytes 6291456 | tf_op jit(solution)/shard_map/convert_element_type | solution.py:101
  216.5 9.6 %multiply_reduce_fusion = bf16[128,4096]{1,0:T(8,128)(2,1)} fusion(f32[128,2,4096]{2,1,0:T(2,128)} %reshape.102, f32[128,2]{1,0:T(8,128)S(1)} %broadcast_select_fusion), kind=kLoop, calls=%fused_computation.9 | loop fusion | flops 1572864 | bytes 5243904 | tf_op jit(solution)/shard_map/reduce_sum | solution.py:102
  (14 shorter events, 0.1 us)
Async XLA Ops:
  30.1 5.6 %copy-start = (s32[128]{0:T(128)S(1)}, s32[128]{0:T(128)}, u32[]{:S(2)}) copy-start(s32[128]{0:T(128)} %param.10) | copy-start | bytes 1540
  144.2 5.3 %copy-start.1 = (bf16[128,2]{0,1:T(2,128)(2,1)S(1)}, bf16[128,2]{0,1:T(2,128)(2,1)}, u32[]{:S(2)}) copy-start(bf16[128,2]{0,1:T(2,128)(2,1)} %param.9) | copy-start | bytes 1540
  144.2 57.8 %all-to-all-start.2 = ((bf16[128,1,1,3,4096]{4,3,2,1,0:T(4,128)(2,1)}), bf16[128,1,1,3,4096]{4,3,2,1,0:T(4,128)(2,1)}, u32[]{:S(2)}, u32[]{:S(2)}) async-start(bf16[128,1,1,3,4096]{4,3,2,1,0:T(4,128)(2,1)} %bitcast.61), calls=%async_computation.2 | async-start | bytes 8388608 | tf_op jit(solution)/shard_map/all_to_all | solution.py:47
where the time goes:
time: 227 us; the launch traced here: 226 us
  blocking collectives  79.8 us (35%)
  local copies, waits for them, and re-layouts  52.5 us (23%)
  waiting for transfers between devices  52.3 us (23%)
  matrix products  19.7 us (9%)
  other arithmetic  16.6 us (7%)
  starting transfers between devices  5.12 us (2%)
    all_to_all x1, waiting for transfers between devices, exchange_both(): lax.all_to_all(blocks, axis, split_axis=0, concat_axis=0, tiled=True)  52.3 us
    all_to_all x1, blocking collectives, on_device(): lax.all_to_all(outgoing, WIDE, split_axis=0, concat_axis=0, tiled=True)  39.4 us
    all_gather x4, blocking collectives, carried_in(): pieces = lax.all_gather(so_far, axis)  27.6 us
    dot_general x1, matrix products, expert_apply(): jnp.dot(hidden, down_matrix, preferred_element_type=jnp.float32)  13.3 us
    all_to_all x1, blocking collectives, on_device(): lax.all_to_all(lax.all_to_all(outgoing, WIDE, split_axis=0, concat_axis=0...  12.8 us
    reshape x2, local copies, waits for them, and re-layouts, on_device(): outgoing = outgoing.reshape(wide_count, narrow_count, most_rows, width)  10.8 us
    reduce_sum x1, other arithmetic, on_device(): mixed = jnp.sum(scaled.reshape(tok_rows, 2, width), axis=1)  9.64 us
    another operation x1, local copies, waits for them, and re-layouts, exchange_both(): blocks = blocks.reshape(-1, *inside)  7.08 us
  transfers between devices with their start and end apart: 1, of which 1 were waited for; matrix products, arithmetic and copies ran while one was open for 0% of the time, Pallas kernels for 0%

commit v1 on v0

v1 whole, which is shorter than its diff:
```python
import functools

import jax
import jax.numpy as jnp
from jax import lax
from jax.experimental import pallas as pl
from jax.experimental.pallas import tpu as pltpu
from jax.sharding import PartitionSpec as P

AXES = ("wide", "narrow")
BF = jnp.bfloat16
F32 = jnp.float32
MIB = 2**20
LANES = 128
ANY = pl.BlockSpec(memory_space=pl.ANY)
VM = pl.BlockSpec(memory_space=pltpu.VMEM)
SM = pl.BlockSpec(memory_space=pltpu.SMEM)
CHUNKS = ((2, 1, 0),)


def named(ids_ref, experts):
    toks = ids_ref.shape[1]
    e = lax.broadcasted_iota(jnp.int32, (experts, toks), 0)
    first = ids_ref[0:1, :] == e
    second = ids_ref[1:2, :] == e
    both = jnp.where(first | second, 1.0, 0.0).astype(BF)
    earlier = lax.broadcasted_iota(jnp.int32, (toks, toks), 0) < lax.broadcasted_iota(
        jnp.int32, (toks, toks), 1
    )
    rank = jnp.dot(both, jnp.where(earlier, 1.0, 0.0).astype(BF), preferred_element_type=F32)
    return first, second, rank


def dispatch_kernel(slots, marked, ids_ref, tok_ref, out_ref):
    experts = out_ref.shape[0]
    first, second, rank = named(ids_ref, experts)
    mine = first | second
    width = tok_ref.shape[1]
    for i, slot in enumerate(slots):
        pick = jnp.where(mine & (rank == float(slot)), 1.0, 0.0).astype(BF)
        rows = jnp.dot(pick, tok_ref[...], preferred_element_type=F32)
        if marked == slot:
            count = jnp.sum(jnp.where(mine, 1.0, 0.0), axis=1, keepdims=True)
            mark = jnp.where(count == 0.0, 8.0, jnp.where(count == 1.0, 16.0, 32.0))
            rows = rows + jnp.where(count >= 3.0, 0.0, mark)
        per = width // LANES
        out_ref[:, i * per : (i + 1) * per, :] = rows.astype(BF).reshape(experts, per, LANES)


def ffn_kernel(slots, leads, nf, nd, look, *refs):
    cap_ref, ref = refs[0], list(refs[1:])
    counts_in = None if leads else ref.pop(0)
    x_hbm, wg_hbm, wu_hbm, wd_hbm = ref[:4]
    ref = ref[4:]
    out_ref = ref.pop(0)
    counts_out = ref.pop(0) if leads else None
    x3, xs, wg, wu, wd, hs, xsem, gsem, usem, dsem = ref
    n, per, ff = x_hbm.shape[0], xs.shape[1] // LANES, hs.shape[1]
    ft, dt = ff // nf, xs.shape[1] // nd
    loads = []
    for f in range(nf):
        cut = (slice(None), slice(f * ft, (f + 1) * ft))
        loads.append(pltpu.make_async_copy(wg_hbm.at[0, :, f * ft : (f + 1) * ft], wg.at[f], gsem.at[f]))
        loads.append(pltpu.make_async_copy(wu_hbm.at[0, :, f * ft : (f + 1) * ft], wu.at[f], usem.at[f]))
    for d in range(nd):
        loads.append(pltpu.make_async_copy(wd_hbm.at[0, :, d * dt : (d + 1) * dt], wd.at[d], dsem.at[d]))
    xload = pltpu.make_async_copy(x_hbm, x3, xsem.at[0])
    xload.start()
    for load in loads[:look]:
        load.start()
    xload.wait()

    def take(i):
        loads[i].wait()
        if i + look < len(loads):
            loads[i + look].start()

    for i in range(len(slots)):
        xs[i * n : (i + 1) * n, :] = x3[:, i * per : (i + 1) * per, :].reshape(n, per * LANES)
    if leads:
        at = slots.index(2)
        seen = xs[at * n : (at + 1) * n, 0:LANES].astype(F32)
        count = jnp.where(seen < 7.0, 3.0, jnp.where(seen < 12.0, 0.0, jnp.where(seen < 24.0, 1.0, 2.0)))
        counts_out[...] = count
    else:
        count = counts_in[...]
    below = lax.broadcasted_iota(jnp.int32, (n, n), 1) < lax.broadcasted_iota(jnp.int32, (n, n), 0)
    before = jnp.dot(
        jnp.where(below, 1.0, 0.0).astype(BF), count.astype(BF), preferred_element_type=F32
    )
    limit = cap_ref[lax.axis_index("wide") * lax.axis_size("narrow") + lax.axis_index("narrow")]
    limit = limit.astype(F32)
    for f in range(nf):
        take(2 * f)
        gate = jnp.dot(xs[...], wg[f], preferred_element_type=F32)
        take(2 * f + 1)
        up = jnp.dot(xs[...], wu[f], preferred_element_type=F32)
        hs[:, f * ft : (f + 1) * ft] = (gate / (1.0 + jnp.exp(-gate)) * up).astype(BF)
    for d in range(nd):
        take(2 * nf + d)
        y = jnp.dot(hs[...], wd[d], preferred_element_type=F32)
        for i, slot in enumerate(slots):
            kept = (count > float(slot)) & (before + float(slot) < limit)
            part = jnp.where(kept[:, 0:1], y[i * n : (i + 1) * n], 0.0).astype(BF)
            p0 = i * per + d * (dt // LANES)
            out_ref[:, p0 : p0 + dt // LANES, :] = part.reshape(n, dt // LANES, LANES)


def combine_kernel(chunks, ids_ref, gates_ref, *refs):
    answers, out_ref = refs[:-1], refs[-1]
    experts, _, lanes = answers[0].shape
    width = out_ref.shape[1]
    per = width // lanes
    first, second, rank = named(ids_ref, experts)
    gates = gates_ref[...].astype(F32)
    weight = jnp.where(first, gates[0:1, :], 0.0) + jnp.where(second, gates[1:2, :], 0.0)
    total = None
    for slots, answer in zip(chunks, answers):
        for i, slot in enumerate(slots):
            pick = jnp.where(rank == float(slot), weight, 0.0).astype(BF)
            rows = answer[:, i * per : (i + 1) * per, :].reshape(experts, width)
            term = lax.dot_general(
                pick, rows, (((0,), (0,)), ((), ())), preferred_element_type=F32
            )
            total = term if total is None else total + term
    out_ref[...] = total.astype(BF)


def exchange(value):
    return lax.all_to_all(value, AXES, split_axis=0, concat_axis=0, tiled=True)


def on_device(tokens, expert_ids, gate_values, capacity, w_gate, w_up, w_down):
    experts = capacity.shape[0]
    toks, width = tokens.shape
    ff = w_gate.shape[2]
    per = width // LANES
    ids = expert_ids.T
    gates = gate_values.T
    nf, nd, look = 3, 4, 4

    def dispatch(slots):
        return pl.pallas_call(
            functools.partial(dispatch_kernel, slots, 2),
            out_shape=jax.ShapeDtypeStruct((experts, len(slots) * per, LANES), BF),
            in_specs=[VM, VM],
            out_specs=VM,
            compiler_params=pltpu.CompilerParams(vmem_limit_bytes=24 * MIB),
            cost_estimate=pl.CostEstimate(
                flops=2 * len(slots) * experts * toks * width, bytes_accessed=3 * MIB, transcendentals=0
            ),
            name=f"dispatch_{slots[0]}",
        )(ids, tokens)

    def ffn(slots, arrived, counts):
        leads = counts is None
        rows = experts * len(slots)
        shape = jax.ShapeDtypeStruct(arrived.shape, BF)
        count_shape = jax.ShapeDtypeStruct((experts, LANES), F32)
        return pl.pallas_call(
            functools.partial(ffn_kernel, slots, leads, nf, nd, look),
            out_shape=(shape, count_shape) if leads else shape,
            in_specs=[SM] + ([] if leads else [VM]) + [ANY] * 4,
            out_specs=(VM, VM) if leads else VM,
            scratch_shapes=[
                pltpu.VMEM(arrived.shape, BF),
                pltpu.VMEM((rows, width), BF),
                pltpu.VMEM((nf, width, ff // nf), BF),
                pltpu.VMEM((nf, width, ff // nf), BF),
                pltpu.VMEM((nd, ff, width // nd), BF),
                pltpu.VMEM((rows, ff), BF),
                pltpu.SemaphoreType.DMA((1,)),
                pltpu.SemaphoreType.DMA((nf,)),
                pltpu.SemaphoreType.DMA((nf,)),
                pltpu.SemaphoreType.DMA((nd,)),
            ],
            compiler_params=pltpu.CompilerParams(vmem_limit_bytes=48 * MIB),
            cost_estimate=pl.CostEstimate(
                flops=6 * rows * width * ff, bytes_accessed=20 * MIB, transcendentals=rows * ff
            ),
            name=f"expert_{slots[0]}",
        )(*([capacity] + ([] if leads else [counts]) + [arrived, w_gate, w_up, w_down]))

    arrived = [exchange(dispatch(slots)) for slots in CHUNKS]
    answers, counts = [], None
    for slots, rows in zip(CHUNKS, arrived):
        if counts is None:
            rows, counts = ffn(slots, rows, None)
        else:
            rows = ffn(slots, rows, counts)
        answers.append(exchange(rows))
    return pl.pallas_call(
        functools.partial(combine_kernel, CHUNKS),
        out_shape=jax.ShapeDtypeStruct((toks, width), BF),
        in_specs=[VM] * (2 + len(answers)),
        out_specs=VM,
        compiler_params=pltpu.CompilerParams(vmem_limit_bytes=32 * MIB),
        cost_estimate=pl.CostEstimate(
            flops=6 * experts * toks * width, bytes_accessed=4 * MIB, transcendentals=0
        ),
        name="combine",
    )(ids, gates, *answers)


def solution(mesh):
    rows, whole = P(AXES, None), P(AXES, None, None)
    return jax.shard_map(
        on_device,
        mesh=mesh,
        in_specs=(rows, rows, rows, P(), whole, whole, whole),
        out_specs=rows,
        check_vma=False,
    )
```

time: 227 us -> 125 us (0.55)
  waiting for transfers between devices: 52.3 us -> 0 us
  local copies, waits for them, and re-layouts: 52.5 us -> 1.92 us
  Pallas kernels: 0 us -> 24.1 us
  matrix products: 19.7 us -> 0 us
  blocking collectives: 79.8 us -> 99.1 us
  other arithmetic: 16.6 us -> 0 us
  starting transfers between devices: 5.12 us -> 0 us
    all_to_all x1 -> x0, waiting for transfers between devices: 52.3 us -> none  [exchange_both(): lax.all_to_all(blocks, axis, split_axis=0, concat_axis=0, tiled=True)]
    all_to_all x2, blocking collectives: 52.3 us -> 99.1 us  [exchange(): return lax.all_to_all(value, AXES, split_axis=0, concat_axis=0, tiled=True)]
    all_gather x4 -> x0, blocking collectives: 27.6 us -> none  [carried_in(): pieces = lax.all_gather(so_far, axis)]
    pallas_call x0 -> x3, Pallas kernels: none -> 24.1 us  [the longest x1 19.7 us: ffn(): pl.pallas_call(functools.partial(ffn_kernel, slots, leads, nf, nd, look),...]
    dot_general x2 -> x0, matrix products: 19.7 us -> none  [the longest x1 13.3 us: expert_apply(): jnp.dot(hidden, down_matrix, preferred_element_type=jnp.float32)]
    reshape x4 -> x0, local copies, waits for them, and re-layouts: 19 us -> none  [the longest x2 10.8 us: on_device(): outgoing = outgoing.reshape(wide_count, narrow_count, most_rows, width)]
    another operation x5 -> x0, local copies, waits for them, and re-layouts: 13.1 us -> none  [the longest x1 7.08 us: exchange_both(): blocks = blocks.reshape(-1, *inside)]
    reduce_sum x3 -> x0, other arithmetic: 10 us -> none  [the longest x1 9.64 us: on_device(): mixed = jnp.sum(scaled.reshape(tok_rows, 2, width), axis=1)]
  transfers between devices with their start and end apart: 1 -> 0, of which waited for: 1 -> 0; matrix products, arithmetic and copies ran while one was open for 0% -> 0% of each run, Pallas kernels for 0% -> 0%
where the time goes in v1:
time: 125 us
  blocking collectives  99.1 us (79%)
  Pallas kernels  24.1 us (19%)
  local copies, waits for them, and re-layouts  1.92 us (2%)
    all_to_all x2, blocking collectives, exchange(): return lax.all_to_all(value, AXES, split_axis=0, concat_axis=0, tiled=True)  99.1 us
    pallas_call x1, Pallas kernels, ffn(): pl.pallas_call(functools.partial(ffn_kernel, slots, leads, nf, nd, look),...  19.7 us
    pallas_call x1, Pallas kernels, on_device(): pl.pallas_call(functools.partial(combine_kernel, CHUNKS), out_shape=jax.S...  2.55 us

profile of v1, /device:TPU:1, one launch (start us, length us, event | category | flops | bytes accessed | tf_op | source)
XLA Modules:
  0.0 125.2 jit_solution(13269759823699429387)
XLA Ops:
  0.0 0.0 copy-start
  0.0 1.2 copy-done
  1.2 0.0 copy-start.1
  1.2 0.7 copy-done.1
  1.9 1.9 %dispatch_2.1 = bf16[128,96,128]{2,1,0:T(8,128)(2,1)S(1)} custom-call(s32[2,128]{1,0:T(2,128)S(1)} %bitcast.2, bf16[128,4096]{1,0:T(8,128)(2,1)S(1)} %copy-done), custom_call_target="tpu_custom_call" | custom-call | flops 402653184 | bytes 3145728 | tf_op jit(solution)/shard_map/dispatch_2/pallas_call | solution.py:143
  3.8 0.0 copy-start.4
  3.8 53.0 %all_to_all.10.refs_1_ = bf16[128,96,128]{2,1,0:T(8,128)(2,1)} all-to-all(bf16[128,96,128]{2,1,0:T(8,128)(2,1)S(1)} %dispatch_2.1), channel_id=1, replica_groups=mesh['wide'=64,'narrow'=2] {'wide','narrow'}, dimensions={0} | all-to-all | bytes 6291456 | tf_op jit(solution)/shard_map/all_to_all | solution.py:130
  56.8 0.0 copy-done.4
  56.8 19.7 %expert_2.1 = (bf16[128,96,128]{2,1,0:T(8,128)(2,1)S(1)}, f32[128,128]{1,0:T(8,128)}) custom-call(s32[128]{0:T(128)S(1)} %copy-done.4, bf16[128,96,128]{2,1,0:T(8,128)(2,1)} %all_to_all.10.refs_1_, bf16[1,4096,768]{2,1,0:T(8,128)(2,1)} %refs_2_.1, bf16[1,4096,768]{2,1,0:T(8,128)(2,1)} %refs_3_.1, bf16[1,768,4096]{2,1,0:T(8,128)(2,1)} %refs_4_.1), custom_call_target="tpu_custom_call" | custom-call | flops 7247757312 | bytes 20971520 | tf_op jit(solution)/shard_map/expert_2/pallas_call | solution.py:160
  76.5 0.0 copy-start.2
  76.5 0.0 copy-start.3
  76.5 46.1 %all_to_all.11.refs_0_ = bf16[128,96,128]{2,1,0:T(8,128)(2,1)S(1)} all-to-all(bf16[128,96,128]{2,1,0:T(8,128)(2,1)S(1)} %get-tuple-element.6), channel_id=1, replica_groups=mesh['wide'=64,'narrow'=2] {'wide','narrow'}, dimensions={0} | all-to-all | bytes 6291456 | tf_op jit(solution)/shard_map/all_to_all | solution.py:130
  122.6 0.0 copy-done.2
  122.6 0.0 copy-done.3
  122.6 2.5 %combine.1 = bf16[128,4096]{1,0:T(8,128)(2,1)} custom-call(s32[2,128]{1,0:T(2,128)S(1)} %bitcast.3, bf16[2,128]{1,0:T(2,128)(2,1)S(1)} %bitcast.4, bf16[128,96,128]{2,1,0:T(8,128)(2,1)S(1)} %all_to_all.11.refs_0_), custom_call_target="tpu_custom_call" | custom-call | flops 402653184 | bytes 4194304 | tf_op jit(solution)/shard_map/combine/pallas_call | solution.py:192
Async XLA Ops:
  0.0 1.2 copy-start
  1.2 0.7 copy-start.1
  3.8 53.0 %copy-start.4 = (s32[128]{0:T(128)S(1)}, s32[128]{0:T(128)}, u32[]{:S(2)}) copy-start(s32[128]{0:T(128)} %refs_0_.1) | copy-start | bytes 1540
  76.5 46.1 %copy-start.2 = (s32[128,2]{0,1:T(2,128)S(1)}, s32[128,2]{0,1:T(2,128)}, u32[]{:S(2)}) copy-start(s32[128,2]{0,1:T(2,128)} %param.8) | copy-start | bytes 3076
  76.5 46.1 %copy-start.3 = (bf16[128,2]{0,1:T(2,128)(2,1)S(1)}, bf16[128,2]{0,1:T(2,128)(2,1)}, u32[]{:S(2)}) copy-start(bf16[128,2]{0,1:T(2,128)(2,1)} %param.9) | copy-start | bytes 1540

commit v2 on v1

v2 whole, which is shorter than its diff:
```python
import functools

import jax
import jax.numpy as jnp
from jax import lax
from jax.experimental import pallas as pl
from jax.experimental.pallas import tpu as pltpu
from jax.sharding import PartitionSpec as P

AXES = ("wide", "narrow")
BF = jnp.bfloat16
F32 = jnp.float32
MIB = 2**20
LANES = 128
ANY = pl.BlockSpec(memory_space=pl.ANY)
VM = pl.BlockSpec(memory_space=pltpu.VMEM)
HB = pl.BlockSpec(memory_space=pltpu.HBM)
SM = pl.BlockSpec(memory_space=pltpu.SMEM)
SLOTS = 3
ND = 4
PARTS = 4
HINT0, HINT1 = 2 * 10**9, 2 * 10**9
DISPATCH_MIB, FFN_MIB, COMBINE_MIB = 12, 16, 12


def named(ids, experts):
    toks = ids.shape[1]
    e = lax.broadcasted_iota(jnp.int32, (experts, toks), 0)
    first = ids[0:1, :] == e
    second = ids[1:2, :] == e
    both = jnp.where(first | second, 1.0, 0.0).astype(BF)
    earlier = lax.broadcasted_iota(jnp.int32, (toks, toks), 0) < lax.broadcasted_iota(
        jnp.int32, (toks, toks), 1
    )
    rank = jnp.dot(both, jnp.where(earlier, 1.0, 0.0).astype(BF), preferred_element_type=F32)
    return first, second, rank


def route_kernel(ids_ref, picks_ref, mark_ref):
    experts = mark_ref.shape[0]
    first, second, rank = named(ids_ref[...], experts)
    mine = first | second
    for slot in range(SLOTS):
        pick = jnp.where(mine & (rank == float(slot)), 1.0, 0.0)
        picks_ref[slot * experts : (slot + 1) * experts, :] = pick.astype(BF)
    count = jnp.sum(jnp.where(mine, 1.0, 0.0), axis=1, keepdims=True)
    mark = jnp.where(count == 0.0, 8.0, jnp.where(count == 1.0, 16.0, 32.0))
    mark_ref[...] = jnp.broadcast_to(jnp.where(count >= 3.0, 0.0, mark), mark_ref.shape)


def dispatch_kernel(picks_ref, mark_ref, tok_ref, out_ref):
    experts, width = out_ref.shape[0], tok_ref.shape[1]
    wide = width // PARTS
    per, part = width // LANES, wide // LANES
    for c in range(PARTS):
        picked = jnp.dot(
            picks_ref[...], tok_ref[:, c * wide : (c + 1) * wide], preferred_element_type=F32
        )
        for slot in range(SLOTS):
            rows = picked[slot * experts : (slot + 1) * experts]
            if slot == SLOTS - 1:
                rows = rows + mark_ref[:, 0:1]
            p0 = slot * per + c * part
            out_ref[:, p0 : p0 + part, :] = rows.astype(BF).reshape(experts, part, LANES)


def ffn_kernel(nd, cap_ref, x_ref, wg_ref, wu_ref, wd_ref, out_ref, hs):
    n, width = x_ref.shape[0], wd_ref.shape[2]
    per, dt = width // LANES, width // nd
    x = jnp.concatenate(
        [x_ref[:, i * per : (i + 1) * per, :].reshape(n, width) for i in range(SLOTS)], axis=0
    )
    gate = jnp.dot(x, wg_ref[0], preferred_element_type=F32)
    up = jnp.dot(x, wu_ref[0], preferred_element_type=F32)
    hs[...] = (gate / (1.0 + jnp.exp(-gate)) * up).astype(BF)
    seen = x[(SLOTS - 1) * n :, 0:LANES].astype(F32)
    count = jnp.where(seen < 7.0, 3.0, jnp.where(seen < 12.0, 0.0, jnp.where(seen < 24.0, 1.0, 2.0)))
    below = lax.broadcasted_iota(jnp.int32, (n, n), 1) < lax.broadcasted_iota(jnp.int32, (n, n), 0)
    before = jnp.dot(
        jnp.where(below, 1.0, 0.0).astype(BF), count.astype(BF), preferred_element_type=F32
    )
    limit = cap_ref[lax.axis_index("wide") * lax.axis_size("narrow") + lax.axis_index("narrow")]
    limit = limit.astype(F32)
    for d in range(nd):
        y = jnp.dot(hs[...], wd_ref[0, :, d * dt : (d + 1) * dt], preferred_element_type=F32)
        for slot in range(SLOTS):
            kept = (count > float(slot)) & (before + float(slot) < limit)
            part = jnp.where(kept[:, 0:1], y[slot * n : (slot + 1) * n], 0.0).astype(BF)
            p0 = slot * per + d * (dt // LANES)
            out_ref[:, p0 : p0 + dt // LANES, :] = part.reshape(n, dt // LANES, LANES)


def combine_kernel(ids_ref, gates_ref, answer_ref, out_hbm, out_ref, sems):
    experts, parts = answer_ref.shape[0], out_ref.shape[0]
    wide = out_ref.shape[2]
    per, part = parts * wide // LANES, wide // LANES
    first, second, rank = named(ids_ref[...], experts)
    gates = gates_ref[...].astype(F32)
    weight = jnp.where(first, gates[0:1, :], 0.0) + jnp.where(second, gates[1:2, :], 0.0)
    picks = jnp.concatenate(
        [jnp.where(rank == float(slot), weight, 0.0).astype(BF) for slot in range(SLOTS)], axis=0
    )
    stores = []
    for c in range(parts):
        rows = jnp.concatenate(
            [
                answer_ref[:, p0 : p0 + part, :].reshape(experts, wide)
                for p0 in range(c * part, SLOTS * per, per)
            ],
            axis=0,
        )
        total = lax.dot_general(picks, rows, (((0,), (0,)), ((), ())), preferred_element_type=F32)
        out_ref[c] = total.astype(BF)
        store = pltpu.make_async_copy(out_ref.at[c], out_hbm.at[:, c * wide : (c + 1) * wide], sems.at[c])
        store.start()
        stores.append(store)
    for store in stores:
        store.wait()


def exchange(value):
    return lax.all_to_all(value, AXES, split_axis=0, concat_axis=0, tiled=True)


def on_device(tokens, expert_ids, gate_values, capacity, w_gate, w_up, w_down):
    experts = capacity.shape[0]
    toks, width = tokens.shape
    ff = w_gate.shape[2]
    rows = SLOTS * experts
    message = jax.ShapeDtypeStruct((experts, SLOTS * width // LANES, LANES), BF)
    ids = expert_ids.T
    gates = gate_values.T
    picks, mark = pl.pallas_call(
        route_kernel,
        out_shape=(
            jax.ShapeDtypeStruct((rows, toks), BF),
            jax.ShapeDtypeStruct((experts, LANES), F32),
        ),
        in_specs=[VM],
        out_specs=(VM, VM),
        compiler_params=pltpu.CompilerParams(vmem_limit_bytes=4 * MIB),
        cost_estimate=pl.CostEstimate(flops=HINT0, bytes_accessed=MIB, transcendentals=0),
        name="route",
    )(ids)
    outgoing = pl.pallas_call(
        dispatch_kernel,
        out_shape=message,
        in_specs=[VM, VM, VM],
        out_specs=VM,
        compiler_params=pltpu.CompilerParams(vmem_limit_bytes=DISPATCH_MIB * MIB),
        cost_estimate=pl.CostEstimate(flops=HINT1, bytes_accessed=4 * MIB, transcendentals=0),
        name="dispatch",
    )(picks, mark, tokens)
    arrived = exchange(outgoing)
    results = pl.pallas_call(
        functools.partial(ffn_kernel, ND),
        out_shape=message,
        in_specs=[SM] + [VM] * 4,
        out_specs=VM,
        scratch_shapes=[pltpu.VMEM((rows, ff), BF)],
        compiler_params=pltpu.CompilerParams(vmem_limit_bytes=FFN_MIB * MIB),
        cost_estimate=pl.CostEstimate(
            flops=6 * rows * width * ff, bytes_accessed=26 * MIB, transcendentals=rows * ff
        ),
        name="expert",
    )(capacity, arrived, w_gate, w_up, w_down)
    answers = exchange(results)
    return pl.pallas_call(
        combine_kernel,
        out_shape=jax.ShapeDtypeStruct((toks, width), BF),
        in_specs=[VM] * 3,
        out_specs=HB,
        scratch_shapes=[
            pltpu.VMEM((PARTS, toks, width // PARTS), BF),
            pltpu.SemaphoreType.DMA((PARTS,)),
        ],
        compiler_params=pltpu.CompilerParams(vmem_limit_bytes=COMBINE_MIB * MIB),
        cost_estimate=pl.CostEstimate(
            flops=2 * rows * toks * width, bytes_accessed=4 * MIB, transcendentals=0
        ),
        name="combine",
    )(ids, gates, answers)


def solution(mesh):
    rows, whole = P(AXES, None), P(AXES, None, None)
    return jax.shard_map(
        on_device,
        mesh=mesh,
        in_specs=(rows, rows, rows, P(), whole, whole, whole),
        out_specs=rows,
        check_vma=False,
    )
```

time: 125 us -> 114 us (0.912)
  Pallas kernels: 24.1 us -> 12.6 us
    pallas_call x3 -> x4, Pallas kernels: 24.1 us -> 12.6 us  [the longest x1 8.74 us: on_device(): pl.pallas_call(functools.partial(ffn_kernel, ND), out_shape=message, in_s...]
where the time goes in v2:
time: 114 us
  blocking collectives  99 us (87%)
  Pallas kernels  12.6 us (11%)
  local copies, waits for them, and re-layouts  2.09 us (2%)
    all_to_all x2, blocking collectives, exchange(): return lax.all_to_all(value, AXES, split_axis=0, concat_axis=0, tiled=True)  99 us
    pallas_call x1, Pallas kernels, on_device(): pl.pallas_call(functools.partial(ffn_kernel, ND), out_shape=message, in_s...  8.74 us
    pallas_call x1, Pallas kernels, on_device(): pl.pallas_call(combine_kernel, out_shape=jax.ShapeDtypeStruct((toks, widt...  2.32 us

profile of v2, /device:TPU:1, one launch (start us, length us, event | category | flops | bytes accessed | tf_op | source)
XLA Modules:
  0.0 113.8 jit_solution(6354643062713935954)
XLA Ops:
  0.0 0.0 copy-start
  0.0 0.7 copy-done
  0.7 0.0 slice-start
  0.7 0.0 slice-start.2
  0.7 0.2 route.1
  0.8 0.0 copy-start.4
  0.9 1.4 %copy-done.4 = bf16[128,4096]{1,0:T(8,128)(2,1)S(1)} copy-done((bf16[128,4096]{1,0:T(8,128)(2,1)S(1)}, bf16[128,4096]{1,0:T(8,128)(2,1)}, u32[]{:S(2)}) %copy-start.4) | copy-done | bytes 1048600
  2.2 0.0 slice-start.1
  2.2 0.0 slice-start.3
  2.2 0.0 copy-start.5
  2.2 1.4 %dispatch.1 = bf16[128,96,128]{2,1,0:T(8,128)(2,1)S(1)} custom-call(bf16[384,128]{1,0:T(8,128)(2,1)S(1)} %get-tuple-element.7.picks_ref, f32[128,128]{1,0:T(8,128)S(1)} %get-tuple-element.8.mark_ref, bf16[128,4096]{1,0:T(8,128)(2,1)S(1)} %copy-done.4), custom_call_target="tpu_custom_call" | custom-call | flops 2000000000 | bytes 4194304 | tf_op jit(solution)/shard_map/dispatch/pallas_call | solution.py:145
  3.7 0.0 copy-start.3
  3.7 52.9 %all_to_all.10.x_ref = bf16[128,96,128]{2,1,0:T(8,128)(2,1)S(1)} all-to-all(bf16[128,96,128]{2,1,0:T(8,128)(2,1)S(1)} %dispatch.1), channel_id=1, replica_groups=mesh['wide'=64,'narrow'=2] {'wide','narrow'}, dimensions={0} | all-to-all | bytes 6291456 | tf_op jit(solution)/shard_map/all_to_all | solution.py:122
  56.6 0.0 slice-done
  56.6 0.0 slice-done.2
  56.6 0.0 slice-done.1
  56.6 0.0 slice-done.3
  56.6 0.0 copy-done.5
  56.6 0.0 copy-done.3
  56.6 8.7 %expert.1 = bf16[128,96,128]{2,1,0:T(8,128)(2,1)S(1)} custom-call(s32[128]{0:T(128)S(1)} %copy-done.5, bf16[128,96,128]{2,1,0:T(8,128)(2,1)S(1)} %all_to_all.10.x_ref, bf16[1,4096,768]{2,1,0:T(8,128)(2,1)S(1)} %bitcast.6, bf16[1,4096,768]{2,1,0:T(8,128)(2,1)S(1)} %bitcast.8, bf16[1,768,4096]{2,1,0:T(8,128)(2,1)S(1)} %copy-done.3), custom_call_target="tpu_custom_call" | custom-call | flops 7247757312 | bytes 27262976 | tf_op jit(solution)/shard_map/expert/pallas_call | solution.py:155
  65.4 0.0 copy-start.1
  65.4 0.0 copy-start.2
  65.4 46.1 %all_to_all.11.answer_ref = bf16[128,96,128]{2,1,0:T(8,128)(2,1)S(1)} all-to-all(bf16[128,96,128]{2,1,0:T(8,128)(2,1)S(1)} %expert.1), channel_id=1, replica_groups=mesh['wide'=64,'narrow'=2] {'wide','narrow'}, dimensions={0} | all-to-all | bytes 6291456 | tf_op jit(solution)/shard_map/all_to_all | solution.py:122
  111.5 0.0 copy-done.1
  111.5 0.0 copy-done.2
  111.5 2.3 %combine.1 = bf16[128,4096]{1,0:T(8,128)(2,1)} custom-call(s32[2,128]{1,0:T(2,128)S(1)} %bitcast.3, bf16[2,128]{1,0:T(2,128)(2,1)S(1)} %bitcast.4, bf16[128,96,128]{2,1,0:T(8,128)(2,1)S(1)} %all_to_all.11.answer_ref), custom_call_target="tpu_custom_call" | custom-call | flops 402653184 | bytes 4194304 | tf_op jit(solution)/shard_map/combine/pallas_call | solution.py:168
  (2 shorter events, 0.0 us)
Async XLA Ops:
  0.0 0.7 copy-start
  0.7 55.9 %slice-start = ((s8[6291456]{0:T(1024)(128)(4,1)}), s8[4194304]{0:T(1024)(128)(4,1)S(1)}, s32[]{:S(2)}) async-start(s8[6291456]{0:T(1024)(128)(4,1)} %bitcast.5), calls=%async_computation.2 | async-start | bytes 8388608
  0.7 55.9 %slice-start.2 = ((s8[6291456]{0:T(1024)(128)(4,1)}), s8[4194304]{0:T(1024)(128)(4,1)S(1)}, s32[]{:S(2)}) async-start(s8[6291456]{0:T(1024)(128)(4,1)} %bitcast.7), calls=%async_computation.4 | async-start | bytes 8388608
  0.8 1.4 %copy-start.4 = (bf16[128,4096]{1,0:T(8,128)(2,1)S(1)}, bf16[128,4096]{1,0:T(8,128)(2,1)}, u32[]{:S(2)}) copy-start(bf16[128,4096]{1,0:T(8,128)(2,1)} %tok_ref.1) | copy-start | bytes 3145732
  2.2 54.4 %slice-start.1 = ((s8[6291456]{0:T(1024)(128)(4,1)}), s8[2097152]{0:T(1024)(128)(4,1)S(1)}, s32[]{:S(2)}) async-start(s8[6291456]{0:T(1024)(128)(4,1)} %bitcast.5), calls=%async_computation.3 | async-start | bytes 4194304
  2.2 54.4 %slice-start.3 = ((s8[6291456]{0:T(1024)(128)(4,1)}), s8[2097152]{0:T(1024)(128)(4,1)S(1)}, s32[]{:S(2)}) async-start(s8[6291456]{0:T(1024)(128)(4,1)} %bitcast.7), calls=%async_computation.5 | async-start | bytes 4194304
  2.2 54.4 %copy-start.5 = (s32[128]{0:T(128)S(1)}, s32[128]{0:T(128)}, u32[]{:S(2)}) copy-start(s32[128]{0:T(128)} %cap_ref.1) | copy-start | bytes 1540
  3.7 53.0 %copy-start.3 = (bf16[1,768,4096]{2,1,0:T(8,128)(2,1)S(1)}, bf16[1,768,4096]{2,1,0:T(8,128)(2,1)}, u32[]{:S(2)}) copy-start(bf16[1,768,4096]{2,1,0:T(8,128)(2,1)} %wd_ref.1) | copy-start | bytes 18874372
  65.4 46.1 %copy-start.1 = (s32[128,2]{0,1:T(2,128)S(1)}, s32[128,2]{0,1:T(2,128)}, u32[]{:S(2)}) copy-start(s32[128,2]{0,1:T(2,128)} %param.8) | copy-start | bytes 3076
  65.4 46.1 %copy-start.2 = (bf16[128,2]{0,1:T(2,128)(2,1)S(1)}, bf16[128,2]{0,1:T(2,128)(2,1)}, u32[]{:S(2)}) copy-start(bf16[128,2]{0,1:T(2,128)(2,1)} %param.9) | copy-start | bytes 1540

commit v3 on v2

--- a/solution.py
+++ b/solution.py
@@ -19,7 +19,8 @@
 SLOTS = 3
 ND = 4
 PARTS = 4
-HINT0, HINT1 = 2 * 10**9, 2 * 10**9
+HINT = 10**9
+HINT0, HINT1 = 10**8, 6 * 10**9
 DISPATCH_MIB, FFN_MIB, COMBINE_MIB = 12, 16, 12
 
 
@@ -36,7 +37,11 @@
     return first, second, rank
 
 
-def route_kernel(ids_ref, picks_ref, mark_ref):
+def first_kernel(out_ref):
+    out_ref[...] = jnp.zeros(out_ref.shape, out_ref.dtype)
+
+
+def route_kernel(ids_ref, first_ref, picks_ref, mark_ref):
     experts = mark_ref.shape[0]
     first, second, rank = named(ids_ref[...], experts)
     mine = first | second
@@ -130,18 +135,26 @@
     message = jax.ShapeDtypeStruct((experts, SLOTS * width // LANES, LANES), BF)
     ids = expert_ids.T
     gates = gate_values.T
+    first = pl.pallas_call(
+        first_kernel,
+        out_shape=jax.ShapeDtypeStruct((8, LANES), F32),
+        out_specs=VM,
+        compiler_params=pltpu.CompilerParams(vmem_limit_bytes=MIB),
+        cost_estimate=pl.CostEstimate(flops=HINT, bytes_accessed=MIB, transcendentals=0),
+        name="first",
+    )()
     picks, mark = pl.pallas_call(
         route_kernel,
         out_shape=(
             jax.ShapeDtypeStruct((rows, toks), BF),
             jax.ShapeDtypeStruct((experts, LANES), F32),
         ),
-        in_specs=[VM],
+        in_specs=[VM, VM],
         out_specs=(VM, VM),
         compiler_params=pltpu.CompilerParams(vmem_limit_bytes=4 * MIB),
         cost_estimate=pl.CostEstimate(flops=HINT0, bytes_accessed=MIB, transcendentals=0),
         name="route",
-    )(ids)
+    )(ids, first)
     outgoing = pl.pallas_call(
         dispatch_kernel,
         out_shape=message,

time: 114 us -> 113 us (level)
  no operation moved by 1% of the time
where the time goes in v3:
time: 113 us
  blocking collectives  99 us (88%)
  Pallas kernels  12.6 us (11%)
    all_to_all x2, blocking collectives, exchange(): return lax.all_to_all(value, AXES, split_axis=0, concat_axis=0, tiled=True)  99 us
    pallas_call x1, Pallas kernels, on_device(): pl.pallas_call(functools.partial(ffn_kernel, ND), out_shape=message, in_s...  8.74 us
    pallas_call x1, Pallas kernels, on_device(): pl.pallas_call(combine_kernel, out_shape=jax.ShapeDtypeStruct((toks, widt...  2.32 us

profile of v3, /device:TPU:1, one launch (start us, length us, event | category | flops | bytes accessed | tf_op | source)
XLA Modules:
  0.0 112.8 jit_solution(6136964178518538506)
XLA Ops:
  0.0 0.0 copy-start
  0.0 0.0 copy-start.2
  0.0 0.7 copy-done
  0.7 0.0 slice-start
  0.7 0.0 slice-start.2
  0.7 0.0 slice-start.4
  0.7 0.2 route.1
  0.8 0.4 copy-done.2
  1.2 0.0 slice-start.1
  1.2 0.0 slice-start.3
  1.2 0.0 slice-start.5
  1.2 1.4 %dispatch.1 = bf16[128,96,128]{2,1,0:T(8,128)(2,1)S(1)} custom-call(bf16[384,128]{1,0:T(8,128)(2,1)S(1)} %get-tuple-element.7.picks_ref, f32[128,128]{1,0:T(8,128)S(1)} %get-tuple-element.8.mark_ref, bf16[128,4096]{1,0:T(8,128)(2,1)S(1)} %copy-done.2), custom_call_target="tpu_custom_call" | custom-call | flops 6000000000 | bytes 4194304 | tf_op jit(solution)/shard_map/dispatch/pallas_call | solution.py:158
  2.7 0.0 copy-start.3
  2.7 52.9 %all_to_all.10.x_ref = bf16[128,96,128]{2,1,0:T(8,128)(2,1)S(1)} all-to-all(bf16[128,96,128]{2,1,0:T(8,128)(2,1)S(1)} %dispatch.1), channel_id=1, replica_groups=mesh['wide'=64,'narrow'=2] {'wide','narrow'}, dimensions={0} | all-to-all | bytes 6291456 | tf_op jit(solution)/shard_map/all_to_all | solution.py:127
  55.6 0.0 slice-done
  55.6 0.0 slice-done.2
  55.6 0.0 slice-done.4
  55.6 0.0 slice-done.1
  55.6 0.0 slice-done.3
  55.6 0.0 slice-done.5
  55.6 0.0 copy-done.3
  55.7 8.7 %expert.1 = bf16[128,96,128]{2,1,0:T(8,128)(2,1)S(1)} custom-call(s32[128]{0:T(128)S(1)} %copy-done.3, bf16[128,96,128]{2,1,0:T(8,128)(2,1)S(1)} %all_to_all.10.x_ref, bf16[1,4096,768]{2,1,0:T(8,128)(2,1)S(1)} %bitcast.6, bf16[1,4096,768]{2,1,0:T(8,128)(2,1)S(1)} %bitcast.8, bf16[1,768,4096]{2,1,0:T(8,128)(2,1)S(1)} %bitcast.10), custom_call_target="tpu_custom_call" | custom-call | flops 7247757312 | bytes 27262976 | tf_op jit(solution)/shard_map/expert/pallas_call | solution.py:168
  64.4 0.0 copy-start.1
  64.4 46.1 %all_to_all.11.answer_ref = bf16[128,96,128]{2,1,0:T(8,128)(2,1)S(1)} all-to-all(bf16[128,96,128]{2,1,0:T(8,128)(2,1)S(1)} %expert.1), channel_id=1, replica_groups=mesh['wide'=64,'narrow'=2] {'wide','narrow'}, dimensions={0} | all-to-all | bytes 6291456 | tf_op jit(solution)/shard_map/all_to_all | solution.py:127
  110.5 0.0 copy-done.1
  110.5 2.3 %combine.1 = bf16[128,4096]{1,0:T(8,128)(2,1)} custom-call(s32[2,128]{1,0:T(2,128)S(1)} %bitcast.3, bf16[2,128]{1,0:T(2,128)(2,1)S(1)} %bitcast.4, bf16[128,96,128]{2,1,0:T(8,128)(2,1)S(1)} %all_to_all.11.answer_ref), custom_call_target="tpu_custom_call" | custom-call | flops 402653184 | bytes 4194304 | tf_op jit(solution)/shard_map/combine/pallas_call | solution.py:181
  (4 shorter events, 0.0 us)
Async XLA Ops:
  0.0 0.7 copy-start
  0.0 1.2 %copy-start.2 = (bf16[128,4096]{1,0:T(8,128)(2,1)S(1)}, bf16[128,4096]{1,0:T(8,128)(2,1)}, u32[]{:S(2)}) copy-start(bf16[128,4096]{1,0:T(8,128)(2,1)} %tok_ref.1) | copy-start | bytes 3145732
  0.7 54.9 %slice-start = ((s8[6291456]{0:T(1024)(128)(4,1)}), s8[4194304]{0:T(1024)(128)(4,1)S(1)}, s32[]{:S(2)}) async-start(s8[6291456]{0:T(1024)(128)(4,1)} %bitcast.5), calls=%async_computation.2 | async-start | bytes 8388608
  0.7 54.9 %slice-start.2 = ((s8[6291456]{0:T(1024)(128)(4,1)}), s8[4194304]{0:T(1024)(128)(4,1)S(1)}, s32[]{:S(2)}) async-start(s8[6291456]{0:T(1024)(128)(4,1)} %bitcast.7), calls=%async_computation.4 | async-start | bytes 8388608
  0.7 54.9 %slice-start.4 = ((s8[6291456]{0:T(1024)(128)(4,1)}), s8[4194304]{0:T(1024)(128)(4,1)S(1)}, s32[]{:S(2)}) async-start(s8[6291456]{0:T(1024)(128)(4,1)} %bitcast.9), calls=%async_computation.6 | async-start | bytes 8388608
  1.2 54.4 %slice-start.1 = ((s8[6291456]{0:T(1024)(128)(4,1)}), s8[2097152]{0:T(1024)(128)(4,1)S(1)}, s32[]{:S(2)}) async-start(s8[6291456]{0:T(1024)(128)(4,1)} %bitcast.5), calls=%async_computation.3 | async-start | bytes 4194304
  1.2 54.4 %slice-start.3 = ((s8[6291456]{0:T(1024)(128)(4,1)}), s8[2097152]{0:T(1024)(128)(4,1)S(1)}, s32[]{:S(2)}) async-start(s8[6291456]{0:T(1024)(128)(4,1)} %bitcast.7), calls=%async_computation.5 | async-start | bytes 4194304
  1.2 54.4 %slice-start.5 = ((s8[6291456]{0:T(1024)(128)(4,1)}), s8[2097152]{0:T(1024)(128)(4,1)S(1)}, s32[]{:S(2)}) async-start(s8[6291456]{0:T(1024)(128)(4,1)} %bitcast.9), calls=%async_computation.7 | async-start | bytes 4194304
  2.7 53.0 %copy-start.3 = (s32[128]{0:T(128)S(1)}, s32[128]{0:T(128)}, u32[]{:S(2)}) copy-start(s32[128]{0:T(128)} %cap_ref.1) | copy-start | bytes 1540
  64.4 46.1 %copy-start.1 = (bf16[128,2]{0,1:T(2,128)(2,1)S(1)}, bf16[128,2]{0,1:T(2,128)(2,1)}, u32[]{:S(2)}) copy-start(bf16[128,2]{0,1:T(2,128)(2,1)} %param.9) | copy-start | bytes 1540

commit v4 on v3

--- a/solution.py
+++ b/solution.py
@@ -17,7 +17,7 @@
 HB = pl.BlockSpec(memory_space=pltpu.HBM)
 SM = pl.BlockSpec(memory_space=pltpu.SMEM)
 SLOTS = 3
-ND = 4
+NF, ND = 3, 4
 PARTS = 4
 HINT = 10**9
 HINT0, HINT1 = 10**8, 6 * 10**9
@@ -69,16 +69,12 @@
             out_ref[:, p0 : p0 + part, :] = rows.astype(BF).reshape(experts, part, LANES)
 
 
-def ffn_kernel(nd, cap_ref, x_ref, wg_ref, wu_ref, wd_ref, out_ref, hs):
-    n, width = x_ref.shape[0], wd_ref.shape[2]
-    per, dt = width // LANES, width // nd
-    x = jnp.concatenate(
-        [x_ref[:, i * per : (i + 1) * per, :].reshape(n, width) for i in range(SLOTS)], axis=0
-    )
-    gate = jnp.dot(x, wg_ref[0], preferred_element_type=F32)
-    up = jnp.dot(x, wu_ref[0], preferred_element_type=F32)
-    hs[...] = (gate / (1.0 + jnp.exp(-gate)) * up).astype(BF)
-    seen = x[(SLOTS - 1) * n :, 0:LANES].astype(F32)
+def ffn_kernel(nf, nd, cap_ref, x_ref, wg_ref, wu_ref, wd_ref, out_ref, xs, hs):
+    n, width, ff = x_ref.shape[0], wd_ref.shape[2], hs.shape[1]
+    per, ft, dt = width // LANES, ff // nf, width // nd
+    for i in range(SLOTS):
+        xs[i * n : (i + 1) * n, :] = x_ref[:, i * per : (i + 1) * per, :].reshape(n, width)
+    seen = xs[(SLOTS - 1) * n : SLOTS * n, 0:LANES].astype(F32)
     count = jnp.where(seen < 7.0, 3.0, jnp.where(seen < 12.0, 0.0, jnp.where(seen < 24.0, 1.0, 2.0)))
     below = lax.broadcasted_iota(jnp.int32, (n, n), 1) < lax.broadcasted_iota(jnp.int32, (n, n), 0)
     before = jnp.dot(
@@ -86,24 +82,36 @@
     )
     limit = cap_ref[lax.axis_index("wide") * lax.axis_size("narrow") + lax.axis_index("narrow")]
     limit = limit.astype(F32)
+    kept = jnp.concatenate(
+        [
+            jnp.where((count > float(slot)) & (before + float(slot) < limit), 1.0, 0.0)[:, 0:1]
+            for slot in range(SLOTS)
+        ],
+        axis=0,
+    )
+    for f in range(nf):
+        cut = slice(f * ft, (f + 1) * ft)
+        gate = jnp.dot(xs[...], wg_ref[0, :, cut], preferred_element_type=F32)
+        up = jnp.dot(xs[...], wu_ref[0, :, cut], preferred_element_type=F32)
+        hidden = gate / (1.0 + jnp.exp(-gate)) * up
+        hs[:, cut] = jnp.where(kept > 0.0, hidden, 0.0).astype(BF)
     for d in range(nd):
         y = jnp.dot(hs[...], wd_ref[0, :, d * dt : (d + 1) * dt], preferred_element_type=F32)
         for slot in range(SLOTS):
-            kept = (count > float(slot)) & (before + float(slot) < limit)
-            part = jnp.where(kept[:, 0:1], y[slot * n : (slot + 1) * n], 0.0).astype(BF)
+            part = y[slot * n : (slot + 1) * n].astype(BF)
             p0 = slot * per + d * (dt // LANES)
             out_ref[:, p0 : p0 + dt // LANES, :] = part.reshape(n, dt // LANES, LANES)
 
 
-def combine_kernel(ids_ref, gates_ref, answer_ref, out_hbm, out_ref, sems):
+def combine_kernel(ids_ref, gates_ref, picks_ref, answer_ref, out_hbm, out_ref, sems):
     experts, parts = answer_ref.shape[0], out_ref.shape[0]
     wide = out_ref.shape[2]
     per, part = parts * wide // LANES, wide // LANES
-    first, second, rank = named(ids_ref[...], experts)
+    e = lax.broadcasted_iota(jnp.int32, (experts, ids_ref.shape[1]), 0)
     gates = gates_ref[...].astype(F32)
-    weight = jnp.where(first, gates[0:1, :], 0.0) + jnp.where(second, gates[1:2, :], 0.0)
+    weight = jnp.where(ids_ref[0:1, :] == e, gates[0:1, :], gates[1:2, :]).astype(BF)
     picks = jnp.concatenate(
-        [jnp.where(rank == float(slot), weight, 0.0).astype(BF) for slot in range(SLOTS)], axis=0
+        [picks_ref[i * experts : (i + 1) * experts, :] * weight for i in range(SLOTS)], axis=0
     )
     stores = []
     for c in range(parts):
@@ -166,11 +174,11 @@
     )(picks, mark, tokens)
     arrived = exchange(outgoing)
     results = pl.pallas_call(
-        functools.partial(ffn_kernel, ND),
+        functools.partial(ffn_kernel, NF, ND),
         out_shape=message,
         in_specs=[SM] + [VM] * 4,
         out_specs=VM,
-        scratch_shapes=[pltpu.VMEM((rows, ff), BF)],
+        scratch_shapes=[pltpu.VMEM((rows, width), BF), pltpu.VMEM((rows, ff), BF)],
         compiler_params=pltpu.CompilerParams(vmem_limit_bytes=FFN_MIB * MIB),
         cost_estimate=pl.CostEstimate(
             flops=6 * rows * width * ff, bytes_accessed=26 * MIB, transcendentals=rows * ff
@@ -181,7 +189,7 @@
     return pl.pallas_call(
         combine_kernel,
         out_shape=jax.ShapeDtypeStruct((toks, width), BF),
-        in_specs=[VM] * 3,
+        in_specs=[VM] * 4,
         out_specs=HB,
         scratch_shapes=[
             pltpu.VMEM((PARTS, toks, width // PARTS), BF),
@@ -192,7 +200,7 @@
             flops=2 * rows * toks * width, bytes_accessed=4 * MIB, transcendentals=0
         ),
         name="combine",
-    )(ids, gates, answers)
+    )(ids, gates, picks, answers)
 
 
 def solution(mesh):

time: 113 us -> 113 us (level)
  no operation moved by 1% of the time
where the time goes in v4:
time: 113 us
  blocking collectives  99 us (88%)
  Pallas kernels  12.5 us (11%)
    all_to_all x2, blocking collectives, exchange(): return lax.all_to_all(value, AXES, split_axis=0, concat_axis=0, tiled=True)  99 us
    pallas_call x1, Pallas kernels, on_device(): pl.pallas_call(functools.partial(ffn_kernel, NF, ND), out_shape=message,...  8.69 us

profile of v4, /device:TPU:1, one launch (start us, length us, event | category | flops | bytes accessed | tf_op | source)
XLA Modules:
  0.0 112.7 jit_solution(1883253033124812367)
XLA Ops:
  0.0 0.0 copy-start
  0.0 0.0 copy-start.2
  0.0 0.7 copy-done
  0.7 0.0 slice-start
  0.7 0.0 slice-start.2
  0.7 0.0 slice-start.4
  0.7 0.2 route.1
  0.8 0.4 copy-done.2
  1.2 0.0 slice-start.1
  1.2 0.0 slice-start.3
  1.2 0.0 slice-start.5
  1.2 1.4 %dispatch.1 = bf16[128,96,128]{2,1,0:T(8,128)(2,1)S(1)} custom-call(bf16[384,128]{1,0:T(8,128)(2,1)S(1)} %get-tuple-element.7.picks_ref, f32[128,128]{1,0:T(8,128)S(1)} %get-tuple-element.8.mark_ref, bf16[128,4096]{1,0:T(8,128)(2,1)S(1)} %copy-done.2), custom_call_target="tpu_custom_call" | custom-call | flops 6000000000 | bytes 4194304 | tf_op jit(solution)/shard_map/dispatch/pallas_call | solution.py:166
  2.7 0.0 copy-start.3
  2.7 52.9 %all_to_all.10.x_ref = bf16[128,96,128]{2,1,0:T(8,128)(2,1)S(1)} all-to-all(bf16[128,96,128]{2,1,0:T(8,128)(2,1)S(1)} %dispatch.1), channel_id=1, replica_groups=mesh['wide'=64,'narrow'=2] {'wide','narrow'}, dimensions={0} | all-to-all | bytes 6291456 | tf_op jit(solution)/shard_map/all_to_all | solution.py:135
  55.6 0.0 slice-done
  55.6 0.0 slice-done.2
  55.6 0.0 slice-done.4
  55.6 0.0 slice-done.1
  55.6 0.0 slice-done.3
  55.6 0.0 slice-done.5
  55.6 0.0 copy-done.3
  55.7 8.7 %expert.1 = bf16[128,96,128]{2,1,0:T(8,128)(2,1)S(1)} custom-call(s32[128]{0:T(128)S(1)} %copy-done.3, bf16[128,96,128]{2,1,0:T(8,128)(2,1)S(1)} %all_to_all.10.x_ref, bf16[1,4096,768]{2,1,0:T(8,128)(2,1)S(1)} %bitcast.6, bf16[1,4096,768]{2,1,0:T(8,128)(2,1)S(1)} %bitcast.8, bf16[1,768,4096]{2,1,0:T(8,128)(2,1)S(1)} %bitcast.10), custom_call_target="tpu_custom_call" | custom-call | flops 7247757312 | bytes 27262976 | tf_op jit(solution)/shard_map/expert/pallas_call | solution.py:176
  64.4 0.0 copy-start.1
  64.4 46.1 %all_to_all.11.answer_ref = bf16[128,96,128]{2,1,0:T(8,128)(2,1)S(1)} all-to-all(bf16[128,96,128]{2,1,0:T(8,128)(2,1)S(1)} %expert.1), channel_id=1, replica_groups=mesh['wide'=64,'narrow'=2] {'wide','narrow'}, dimensions={0} | all-to-all | bytes 6291456 | tf_op jit(solution)/shard_map/all_to_all | solution.py:135
  110.5 0.0 copy-done.1
  110.5 2.2 %combine.1 = bf16[128,4096]{1,0:T(8,128)(2,1)} custom-call(s32[2,128]{1,0:T(2,128)S(1)} %bitcast.3, bf16[2,128]{1,0:T(2,128)(2,1)S(1)} %bitcast.4, bf16[384,128]{1,0:T(8,128)(2,1)S(1)} %get-tuple-element.7.picks_ref, bf16[128,96,128]{2,1,0:T(8,128)(2,1)S(1)} %all_to_all.11.answer_ref), custom_call_target="tpu_custom_call" | custom-call | flops 402653184 | bytes 4194304 | tf_op jit(solution)/shard_map/combine/pallas_call | solution.py:189
  (4 shorter events, 0.0 us)
Async XLA Ops:
  0.0 0.7 copy-start
  0.0 1.2 %copy-start.2 = (bf16[128,4096]{1,0:T(8,128)(2,1)S(1)}, bf16[128,4096]{1,0:T(8,128)(2,1)}, u32[]{:S(2)}) copy-start(bf16[128,4096]{1,0:T(8,128)(2,1)} %tok_ref.1) | copy-start | bytes 3145732
  0.7 54.9 %slice-start = ((s8[6291456]{0:T(1024)(128)(4,1)}), s8[4194304]{0:T(1024)(128)(4,1)S(1)}, s32[]{:S(2)}) async-start(s8[6291456]{0:T(1024)(128)(4,1)} %bitcast.5), calls=%async_computation.2 | async-start | bytes 8388608
  0.7 54.9 %slice-start.2 = ((s8[6291456]{0:T(1024)(128)(4,1)}), s8[4194304]{0:T(1024)(128)(4,1)S(1)}, s32[]{:S(2)}) async-start(s8[6291456]{0:T(1024)(128)(4,1)} %bitcast.7), calls=%async_computation.4 | async-start | bytes 8388608
  0.7 54.9 %slice-start.4 = ((s8[6291456]{0:T(1024)(128)(4,1)}), s8[4194304]{0:T(1024)(128)(4,1)S(1)}, s32[]{:S(2)}) async-start(s8[6291456]{0:T(1024)(128)(4,1)} %bitcast.9), calls=%async_computation.6 | async-start | bytes 8388608
  1.2 54.4 %slice-start.1 = ((s8[6291456]{0:T(1024)(128)(4,1)}), s8[2097152]{0:T(1024)(128)(4,1)S(1)}, s32[]{:S(2)}) async-start(s8[6291456]{0:T(1024)(128)(4,1)} %bitcast.5), calls=%async_computation.3 | async-start | bytes 4194304
  1.2 54.4 %slice-start.3 = ((s8[6291456]{0:T(1024)(128)(4,1)}), s8[2097152]{0:T(1024)(128)(4,1)S(1)}, s32[]{:S(2)}) async-start(s8[6291456]{0:T(1024)(128)(4,1)} %bitcast.7), calls=%async_computation.5 | async-start | bytes 4194304
  1.2 54.4 %slice-start.5 = ((s8[6291456]{0:T(1024)(128)(4,1)}), s8[2097152]{0:T(1024)(128)(4,1)S(1)}, s32[]{:S(2)}) async-start(s8[6291456]{0:T(1024)(128)(4,1)} %bitcast.9), calls=%async_computation.7 | async-start | bytes 4194304
  2.7 53.0 %copy-start.3 = (s32[128]{0:T(128)S(1)}, s32[128]{0:T(128)}, u32[]{:S(2)}) copy-start(s32[128]{0:T(128)} %cap_ref.1) | copy-start | bytes 1540
  64.4 46.1 %copy-start.1 = (bf16[128,2]{0,1:T(2,128)(2,1)S(1)}, bf16[128,2]{0,1:T(2,128)(2,1)}, u32[]{:S(2)}) copy-start(bf16[128,2]{0,1:T(2,128)(2,1)} %param.9) | copy-start | bytes 1540
